TPU v7x, 32 devices: a whole 2x2x4 slice. The times are simulated.
32 devices in a mesh: groups: 2 (over x), elem: 16 (over z, y, core).
Axes of the slice: x: 2, y: 2, z: 4, core: 2. Of those that a mesh axis runs over, the one named last changes fastest.
Arguments:
- snapshots: float32 [2, 4096, 16384], P(None, ('groups', 'elem')), parts along dimension 1, may hold values from -6 to 6
- delays: float32 [384, 2048], replicated, may hold values from -3 to 3
- element_order: int32 [4096], P('groups'), parts along dimension 0, may hold values from 0 to 2047, each once
- beam_table: int32 [512], P('groups'), parts along dimension 0, may hold values from 0 to 383
- band_len: int32 [8], replicated, may hold values from 1 to 4, 16 in all
Outputs:
- beams: float32 [16384, 2, 512], P('elem', None, 'groups'), parts along dimension 2
- power_db: float32 [8, 512], P(None, 'groups'), parts along dimension 1
There are 2 independent parts, one for each index of `groups`. A program takes and returns all parts, laid end to end along the dimension named above; an argument that names none is the same for every part. Nothing has to cross between parts.
Inputs may be any that keep to these rules, and one draw needn't show every extreme that they name: `element_order`: each of 0 to 2047 appears once. `band_len`: the entries sum to 16.
All inputs are finite; a program needn't handle non-finite values.
Results may differ from a plain program's by a relative error of at most 0.0003.
Values sent between devices are 32-bit elements; how exact they have to be, the bound alone decides.
A program may use at most 128 MiB of HBM per device.

v0:
```python
import math

import jax
import jax.numpy as jnp
from jax import lax
from jax.sharding import PartitionSpec as P

epsilon = 1e-06


def band_of(band_len, position, unit_count):
    band_ends = jnp.cumsum(band_len)
    band_index = jnp.sum((band_ends <= position).astype(jnp.int32))
    selector = jnp.arange(band_len.shape[0], dtype=jnp.int32) == band_index
    band_size = jnp.sum(jnp.where(selector, band_len, 0))
    band_start = jnp.sum(jnp.where(selector, band_ends, 0)) - band_size
    frequency = (band_start.astype(jnp.float32) + 0.5 * band_size.astype(jnp.float32)) / float(
        unit_count
    )
    return (frequency, band_size, selector.astype(jnp.float32))


def steering(delays, element_order, beam_table, frequency):
    delay_rows = jnp.take(delays, beam_table, axis=0)
    delay_rows = jnp.take(delay_rows, element_order, axis=1)
    phases = 2.0 * math.pi * frequency * delay_rows
    scaling = float(delays.shape[1]) ** (-0.5)
    cosines = jnp.cos(phases) * scaling
    sines = -jnp.sin(phases) * scaling
    upper_rows = jnp.concatenate([cosines.T, sines.T], axis=1)
    lower_rows = jnp.concatenate([-sines.T, cosines.T], axis=1)
    return jnp.concatenate([upper_rows, lower_rows], axis=0)


def project(arrived, weights):
    columns = arrived.shape[2]
    stacked = arrived.reshape(2 * arrived.shape[1], columns)
    return lax.dot_general(
        stacked,
        weights,
        (((0,), (0,)), ((), ())),
        precision=lax.Precision.HIGHEST,
        preferred_element_type=jnp.float32,
    )


def local(snapshots, delays, element_order, beam_table, band_len):
    unit_count = lax.axis_size("elem")
    position = lax.axis_index("elem")
    frequency, band_size, selector = band_of(band_len, position, unit_count)
    weights = steering(delays, element_order, beam_table, frequency)
    beam_count = beam_table.shape[0]
    local_elems = snapshots.shape[1]
    unit_cols = snapshots.shape[2] // unit_count
    divided = snapshots.reshape(2, local_elems, unit_count, unit_cols)
    pieces = lax.all_to_all(divided, "elem", split_axis=2, concat_axis=1, tiled=True)
    formed = project(pieces.reshape(2, pieces.shape[1], pieces.shape[3]), weights)
    column_count = formed.shape[0]
    squares = jnp.sum(formed * formed, axis=0)
    power_mean = (squares[:beam_count] + squares[beam_count:]) / (
        band_size.astype(jnp.float32) * column_count
    )
    partial_value = selector[:, None] * power_mean[None, :]
    summed = lax.psum(partial_value, "elem")
    decibels = 10.0 * jnp.log10(summed + epsilon)
    return (formed.reshape(column_count, 2, beam_count), decibels)


def solution(mesh):
    return jax.shard_map(
        local,
        mesh=mesh,
        in_specs=(P(None, ("groups", "elem"), None), P(), P("groups"), P("groups"), P()),
        out_specs=(P("elem", None, "groups"), P(None, "groups")),
        check_vma=False,
    )
```

profile of v0, /device:TPU:0, one launch (start us, length us, event | category | flops | bytes accessed | tf_op | source)
XLA Modules:
  0.0 488.5 jit_solution(5320041055812886282)
XLA Ops:
  0.6 0.0 copy-start
  0.6 17.6 %copy.16 = f32[2,128,16384]{1,2,0:T(8,128)} copy(f32[2,128,16384]{2,1,0:T(8,128)} %param.5) | data formatting | bytes 33554432 | tf_op args[0]
  18.2 11.3 %copy.17 = f32[2,128,16,1024]{1,3,0,2:T(8,128)} copy(f32[2,128,16,1024]{1,3,2,0:T(8,128)} %bitcast.19) | data formatting | bytes 33554432 | tf_op jit(solution)/shard_map/reshape | solution.py:55
  29.5 0.0 copy-start.3
  29.5 7.6 %all-to-all-start = ((f32[2,128,16,1024]{1,3,0,2:T(8,128)}), f32[2,128,16,1024]{1,3,0,2:T(8,128)}, u32[]{:S(2)}, u32[]{:S(2)}) async-start(f32[2,128,16,1024]{1,3,0,2:T(8,128)} %copy.17), calls=%async_computation | async-start | bytes 33554432 | tf_op jit(solution)/shard_map/all_to_all | solution.py:56
  37.1 0.0 copy-done.3
  37.2 0.0 copy-done
  37.2 2.7 gather_fusion
  39.9 3.1 broadcast_select_fusion
  43.0 0.0 copy-start.4
  43.0 0.0 copy-start.2
  43.0 1.9 copy.15
  44.9 0.0 copy-done.4
  44.9 0.2 reduce-window.9
  45.1 0.6 fusion.10
  45.8 1.3 fusion.11
  49.1 0.0 copy-done.2
  49.1 8.6 %gather_fusion.1 = f32[2048,256]{1,0:T(8,128)} fusion(f32[256,2048]{0,1:T(8,128)S(1)} %copy.15, s32[2048]{0:T(1024)S(1)} %fusion.9), kind=kCustom, calls=%fused_computation.1 | custom fusion | bytes 4202496 | tf_op jit(solution)/shard_map/jit(_take)/gather | solution.py:25
  57.7 0.6 fusion.12
  58.4 10.9 %fusion.14 = (f32[2048,256]{1,0:T(8,128)S(1)}, f32[2048,256]{1,0:T(8,128)}, f32[2048,256]{1,0:T(8,128)}) fusion(f32[2048,256]{1,0:T(8,128)} %gather_fusion.1, pred[2048]{0:T(1024)(128)(4,1)S(1)} %compare_and_fusion, f32[]{:T(128)S(6)} %mul_shard_map.7), kind=kLoop, calls=%fused_computation.33 | loop fusion | flops 3145728 | bytes 8390660 | tf_op jit(solution)/shard_map/neg | solution.py:31
  69.3 264.4 %all-to-all-done = f32[2,128,16,1024]{1,3,0,2:T(8,128)} async-done(((f32[2,128,16,1024]{1,3,0,2:T(8,128)}), f32[2,128,16,1024]{1,3,0,2:T(8,128)}, u32[]{:S(2)}, u32[]{:S(2)}) %all-to-all-start) | async-done | bytes 16777248 | tf_op jit(solution)/shard_map/all_to_all | solution.py:56
  333.8 18.0 %copy.18 = f32[2,128,16,1024]{3,1,2,0:T(8,128)} copy(f32[2,128,16,1024]{1,3,0,2:T(8,128)} %all-to-all-done) | data formatting | bytes 33554432 | tf_op jit(solution)/shard_map/all_to_all | solution.py:56
  351.8 33.0 %fusion.8 = (f32[512]{0:T(512)S(1)}, f32[512,1024]{1,0:T(8,128)}) fusion(f32[4096,1024]{1,0:T(8,128)} %bitcast.20, f32[2048,256]{1,0:T(8,128)} %get-tuple-element.12, f32[2048,256]{1,0:T(8,128)S(1)} %get-tuple-element.10, f32[2048,256]{1,0:T(8,128)} %get-tuple-element.11), kind=kOutput, calls=%fused_computation.11 | convolution fusion | flops 25777143808 | bytes 25167872 | tf_op jit(solution)/shard_map/dot_general | solution.py:38
  384.7 0.0 copy-start.1
  384.7 4.3 copy.19
  389.0 0.1 broadcast_multiply_fusion
  389.1 98.8 %psum.7 = f32[8,256]{1,0:T(8,128)S(1)} all-reduce(f32[8,256]{1,0:T(8,128)S(1)} %broadcast_multiply_fusion), channel_id=1, replica_groups=mesh['groups'=2,'elem'=16] {'elem'}, use_global_device_ids=true, to_apply=%region_5.6 | all-reduce | flops 2048 | bytes 16384 | tf_op jit(solution)/shard_map/psum | solution.py:64
  487.9 0.6 log_multiply_fusion
  488.5 0.0 copy-done.1
  (6 shorter events, 0.0 us)
Async XLA Ops:
  0.6 36.5 %copy-start = (f32[384,2048]{1,0:T(8,128)S(1)}, f32[384,2048]{1,0:T(8,128)}, u32[]{:S(2)}) copy-start(f32[384,2048]{1,0:T(8,128)} %param.6) | copy-start | bytes 9437188
  29.5 7.6 %copy-start.3 = (s32[256]{0:T(256)S(1)}, s32[256]{0:T(256)}, u32[]{:S(2)}) copy-start(s32[256]{0:T(256)} %param.8) | copy-start | bytes 3076
  29.5 304.2 %all-to-all-start = ((f32[2,128,16,1024]{1,3,0,2:T(8,128)}), f32[2,128,16,1024]{1,3,0,2:T(8,128)}, u32[]{:S(2)}, u32[]{:S(2)}) async-start(f32[2,128,16,1024]{1,3,0,2:T(8,128)} %copy.17), calls=%async_computation | async-start | bytes 33554432 | tf_op jit(solution)/shard_map/all_to_all | solution.py:56
  43.0 2.0 copy-start.4
  43.0 6.1 %copy-start.2 = (s32[2048]{0:T(1024)S(1)}, s32[2048]{0:T(1024)}, u32[]{:S(2)}) copy-start(s32[2048]{0:T(1024)} %param.7) | copy-start | bytes 24580
  384.7 103.8 %copy-start.1 = (f32[384,2048]{1,0:T(8,128)S(1)}, f32[384,2048]{1,0:T(8,128)}, u32[]{:S(2)}) copy-start(f32[384,2048]{1,0:T(8,128)} %param.6) | copy-start | bytes 9437188
where the time goes:
time: 489 us; the launch traced here: 488 us
  waiting for transfers between devices  264 us (54%)
  blocking collectives  98.8 us (20%)
  local copies, waits for them, and re-layouts  64.4 us (13%)
  matrix products  33 us (7%)
  other arithmetic  17.6 us (4%)
  starting transfers between devices  7.6 us (2%)
    all_to_all x1, waiting for transfers between devices, local(): lax.all_to_all(divided, 'elem', split_axis=2, concat_axis=1, tiled=True)  264 us
    psum x1, blocking collectives, local(): summed = lax.psum(partial_value, 'elem')  98.8 us
    dot_general x1, matrix products, project(): lax.dot_general(stacked, weights, (((0,), (0,)), ((), ())), precision=lax...  33 us
    unnamed x12, local copies, waits for them, and re-layouts  21.9 us
    all_to_all x1, local copies, waits for them, and re-layouts, local(): lax.all_to_all(divided, 'elem', split_axis=2, concat_axis=1, tiled=True)  18 us
    reshape x1, local copies, waits for them, and re-layouts, local(): divided = snapshots.reshape(2, local_elems, unit_count, unit_cols)  11.3 us
    neg x1, other arithmetic, steering(): lower_rows = jnp.concatenate([-sines.T, cosines.T], axis=1)  10.9 us
  transfers between devices with their start and end apart: 1, of which 1 were waited for; matrix products, arithmetic and copies ran while one was open for 6% of the time, Pallas kernels for 0%

commit v1 on v0

--- a/solution.py
+++ b/solution.py
@@ -1,11 +1,16 @@
+import functools
 import math
 
 import jax
 import jax.numpy as jnp
 from jax import lax
+from jax.experimental import pallas as pl
+from jax.experimental.pallas import tpu as pltpu
 from jax.sharding import PartitionSpec as P
 
 epsilon = 1e-06
+SIDE = 2
+RING = 4
 
 
 def band_of(band_len, position, unit_count):
@@ -18,6 +23,362 @@
         unit_count
     )
     return (frequency, band_size, selector.astype(jnp.float32))
+
+
+def sincos(turns):
+    reduced = turns - jnp.floor(turns + 0.5)
+    x = reduced * math.pi
+    q = x * x
+    sin_terms = [(-1.0) ** i / math.factorial(2 * i + 1) for i in range(7)]
+    cos_terms = [(-1.0) ** i / math.factorial(2 * i) for i in range(8)]
+    s = jnp.full_like(q, sin_terms[-1])
+    for term in sin_terms[-2::-1]:
+        s = s * q + term
+    s = s * x
+    c = jnp.full_like(q, cos_terms[-1])
+    for term in cos_terms[-2::-1]:
+        c = c * q + term
+    return 2.0 * s * c, 1.0 - 2.0 * s * s
+
+
+def split2(v):
+    high = v.astype(jnp.bfloat16)
+    return high, (v - high.astype(jnp.float32)).astype(jnp.bfloat16)
+
+
+def split3(v):
+    high = v.astype(jnp.bfloat16)
+    rest = v - high.astype(jnp.float32)
+    middle = rest.astype(jnp.bfloat16)
+    return high, middle, (rest - middle.astype(jnp.float32)).astype(jnp.bfloat16)
+
+
+def kernel(
+    n, freq, x, delays, order, table, out, power,
+    g1, dt, xa, xb, xz, pa, pb, ra1, ra2, rb, ry2, pw,
+    own_a, own_b, sa_s, sa_r, sb_s, sb_r, sy_s, sy_r, sz_s, sz_r,
+    b_s, b_r, a1_s, a1_r, a2_s, a2_r, y2_s, y2_r, p_s, p_r,
+):
+    me = lax.axis_index("elem")
+    core = me % SIDE
+    y = (me // SIDE) % SIDE
+    z = me // (SIDE * SIDE)
+    unit_cols = x.shape[2] // n
+    quarter = unit_cols // 4
+    half_cols = 2 * quarter
+    beams = table.shape[0]
+    scaling = float(delays.shape[1]) ** (-0.5)
+    hop = (2, 3, 1, 0)
+
+    def dev(zz, yy, cc):
+        return ((zz % RING) * SIDE + yy % SIDE) * SIDE + cc % SIDE
+
+    barrier = pltpu.get_barrier_semaphore()
+
+    def greet(k, carry):
+        pl.semaphore_signal(barrier, inc=1, device_id={"elem": (me + k) % n},
+                            device_id_type=pl.DeviceIdType.MESH)
+        return carry
+
+    lax.fori_loop(1, n, greet, 0)
+    pl.semaphore_wait(barrier, n - 1)
+
+    def remote(src, dst, send, recv, target):
+        return pltpu.make_async_remote_copy(
+            src_ref=src, dst_ref=dst, send_sem=send, recv_sem=recv,
+            device_id={"elem": target}, device_id_type=pl.DeviceIdType.MESH)
+
+    def cols(unit, start, size):
+        return x.at[:, :, pl.ds(pl.multiple_of(unit * unit_cols + start, 128), size)]
+
+    sends = []
+
+    def go(copy):
+        copy.start()
+        sends.append(copy)
+        return copy
+
+    cz = {}
+    for yr in (1, 0):
+        for r in (0, 1):
+            for d in (0, 1):
+                unit = dev(z + 2, y + yr, core + r)
+                cz[d, r, yr] = go(remote(
+                    cols(unit, half_cols + d * quarter, quarter), xz.at[d, r, yr],
+                    sz_s.at[d, r, yr], sz_r.at[d, r, yr], dev(z + 3 - 2 * d, y, core + r)))
+    cy = {}
+    for j in range(4):
+        for r in (0, 1):
+            unit = dev(z + hop[j], y + 1, core + r)
+            cy[r, j] = go(remote(
+                cols(unit, 0, half_cols), xa.at[2 + r, j],
+                sy_s.at[r, j], sy_r.at[r, j], dev(z, y + 1, core + r)))
+    ca, cb, la, lb = {}, {}, {}, {}
+    for jj in range(3):
+        for yr in (1, 0):
+            unit = dev(z + hop[jj + 1], y + yr, core + 1)
+            cb[jj, yr] = go(remote(
+                cols(unit, half_cols, half_cols), xb.at[1, jj, yr],
+                sb_s.at[jj, yr], sb_r.at[jj, yr], dev(z, y, core + 1)))
+            lb[jj, yr] = pltpu.make_async_copy(
+                cols(dev(z + hop[jj + 1], y + yr, core), half_cols, half_cols),
+                xb.at[0, jj, yr], own_b.at[jj, yr])
+            lb[jj, yr].start()
+    for j in range(4):
+        ca[j] = go(remote(
+            cols(dev(z + hop[j], y, core + 1), 0, half_cols), xa.at[1, j],
+            sa_s.at[j], sa_r.at[j], dev(z, y, core + 1)))
+        la[j] = pltpu.make_async_copy(
+            cols(dev(z + hop[j], y, core), 0, half_cols), xa.at[0, j], own_a.at[j])
+        la[j].start()
+
+    beam_hot = jnp.where(
+        lax.broadcasted_iota(jnp.int32, (beams, delays.shape[0]), 1) == table[...], 1.0, 0.0
+    ).astype(jnp.bfloat16)
+    step = 512 if delays.shape[1] % 512 == 0 else delays.shape[1]
+
+    def pick_beams(i, carry):
+        span = pl.ds(pl.multiple_of(i * step, step), step)
+        parts = split3(delays[:, span])
+        rows = [jnp.dot(beam_hot, part, preferred_element_type=jnp.float32) for part in parts]
+        for m, part in enumerate(rows):
+            g1[m * beams:(m + 1) * beams, span] = part.astype(jnp.bfloat16)
+        return carry
+
+    lax.fori_loop(0, delays.shape[1] // step, pick_beams, 0)
+
+    def pick_elems(s, carry):
+        r, g = s % 2, s // 2
+        q = dev(z + (g // 2) * (1 + 2 * (g % 2)), y + (g % 2) * (1 - g // 2), core + r)
+        row = order[q]
+        hot = jnp.where(
+            lax.broadcasted_iota(jnp.int32, (delays.shape[1], row.shape[1]), 0) == row, 1.0, 0.0
+        ).astype(jnp.bfloat16)
+        got = jnp.dot(g1[...], hot, preferred_element_type=jnp.float32)
+        dt[s] = got[:beams] + got[beams:2 * beams] + got[2 * beams:]
+        return carry
+
+    lax.fori_loop(0, 8, pick_elems, 0)
+
+    def term(xv, s, f):
+        sine, cosine = sincos(f * dt[s])
+        ch, cl = split2(cosine * scaling)
+        sh, sl = split2(sine * scaling)
+        wh = jnp.concatenate(
+            [jnp.concatenate([ch, sh], axis=1), jnp.concatenate([-sh, ch], axis=1)], axis=0)
+        wl = jnp.concatenate(
+            [jnp.concatenate([cl, sl], axis=1), jnp.concatenate([-sl, cl], axis=1)], axis=0)
+        xh, xl = split2(xv.reshape(xv.shape[0] * xv.shape[1], xv.shape[2]))
+        dot = functools.partial(jnp.dot, preferred_element_type=jnp.float32)
+        return dot(wh, xh) + (dot(wh, xl) + dot(wl, xh))
+
+    def part(h):
+        return pl.ds(pl.multiple_of(h * quarter, 128), quarter)
+
+    def chip_terms(jj, yr, h, f):
+        pb[jj, yr, h] = term(xb[0, jj, yr, :, :, part(h)], 0, f)
+
+        def add(s, carry):
+            pb[jj, yr, h] += term(xb[s, jj, yr, :, :, part(h)], s, f)
+            return carry
+
+        lax.fori_loop(1, 2, add, 0)
+
+    def b_copy(jj, yr, h):
+        return remote(pb.at[jj, yr, h], rb.at[jj, yr, h], b_s.at[jj, yr, h], b_r.at[jj, yr, h],
+                      dev(z + 3 - 2 * jj, y, core))
+
+    def b_freq(jj, yr):
+        return freq[dev(z + 3 - 2 * jj, y + yr, core)]
+
+    for jj in (0, 1):
+        for yr in (1, 0):
+            lb[jj, yr].wait()
+            cb[jj, yr].wait_recv()
+
+    def b_alone(t, carry):
+        jj, yr = t % 2, 1 - t // 2
+        chip_terms(jj, yr, 1 - jj, b_freq(jj, yr))
+        b_copy(jj, yr, 1 - jj).start()
+        return carry
+
+    lax.fori_loop(0, 4, b_alone, 0)
+    for yr in (1, 0):
+        for r in (0, 1):
+            for d in (0, 1):
+                cz[d, r, yr].wait_recv()
+
+    def b_joint(t, carry):
+        jj, yr = t % 2, 1 - t // 2
+        f = b_freq(jj, yr)
+        chip_terms(jj, yr, jj, f)
+
+        def add(r, inner):
+            pb[jj, yr, jj] += term(xz[jj, r, yr], 4 + 2 * jj + r, f)
+            return inner
+
+        lax.fori_loop(0, 2, add, 0)
+        b_copy(jj, yr, jj).start()
+        return carry
+
+    lax.fori_loop(0, 4, b_joint, 0)
+
+    def a_slot(j):
+        la[j].wait()
+        ca[j].wait_recv()
+        for r in (0, 1):
+            cy[r, j].wait_recv()
+        f = freq[dev(z + hop[j], y, core)]
+        for h in (0, 1):
+            pa[j, h] = jnp.zeros_like(pa[j, h])
+
+        def add(t, carry):
+            h, s = t % 2, t // 2
+            pa[j, h] += term(xa[s, j, :, :, part(h)], s, f)
+            return carry
+
+        lax.fori_loop(0, 8, add, 0)
+
+    a_slot(0)
+    ca1 = [go(remote(pa.at[0, h], ra1.at[h], a1_s.at[h], a1_r.at[h], dev(z + 3 - 2 * h, y, core)))
+           for h in (0, 1)]
+
+    for yr in (1, 0):
+        lb[2, yr].wait()
+        cb[2, yr].wait_recv()
+
+    def b_own(t, carry):
+        yr, h = t % 2, t // 2
+        chip_terms(2, yr, h, freq[dev(z, y + yr, core)])
+        return carry
+
+    lax.fori_loop(0, 4, b_own, 0)
+
+    ca2 = {}
+
+    def a_send(d, h):
+        ca2[d, h] = go(remote(pa.at[1 + d, h], ra2.at[d, h], a2_s.at[d, h], a2_r.at[d, h],
+                              dev(z + 3 - 2 * d, y, core)))
+
+    def a_joint(d):
+        ca1[d].wait_recv()
+        pa[1 + d, d] += ra1[d]
+        a_send(d, d)
+
+    a_slot(1)
+    a_send(0, 1)
+    a_joint(0)
+    a_slot(2)
+    a_send(1, 0)
+    a_joint(1)
+
+    def b_gather(yr):
+        for h in (0, 1):
+            for jj in (0, 1):
+                b_copy(jj, yr, h).wait_recv()
+            pb[2, yr, h] += rb[0, yr, h] + rb[1, yr, h]
+
+    cy2 = []
+    b_gather(1)
+    for h in (0, 1):
+        cy2.append(go(remote(pb.at[2, 1, h], ry2.at[h], y2_s.at[h], y2_r.at[h],
+                             dev(z, y + 1, core))))
+    b_gather(0)
+    a_slot(3)
+
+    for h in (0, 1):
+        for d in (0, 1):
+            ca2[d, h].wait_recv()
+        got = (pa[3, h] + ra2[0, h] + ra2[1, h]).T
+        out[h * quarter:(h + 1) * quarter, :] = got
+        squares = jnp.sum(got * got, axis=0, keepdims=True)
+        total = squares if h == 0 else total + squares
+    for h in (0, 1):
+        cy2[h].wait_recv()
+        got = (pb[2, 0, h] + ry2[h]).T
+        out[half_cols + h * quarter:half_cols + (h + 1) * quarter, :] = got
+        total = total + jnp.sum(got * got, axis=0, keepdims=True)
+    both = total[:, :beams] + total[:, beams:]
+    pw[0] = jnp.broadcast_to(both, pw.shape[1:])
+
+    def p_copy(k):
+        return remote(pw.at[0], pw.at[k], p_s.at[k], p_r.at[k], (me + k) % n)
+
+    def p_start(k, carry):
+        p_copy(k).start()
+        return carry
+
+    def p_wait(k, carry):
+        p_copy(k).wait()
+        return carry
+
+    lax.fori_loop(1, n, p_start, 0)
+    for copy in sends:
+        copy.wait_send()
+
+    def b_drain(t, carry):
+        b_copy(t // 4, (t // 2) % 2, t % 2).wait_send()
+        return carry
+
+    lax.fori_loop(0, 8, b_drain, 0)
+    lax.fori_loop(1, n, p_wait, 0)
+    power[...] = pw[...]
+
+
+def local_ring(n, snapshots, delays, element_order, beam_table, band_len):
+    local_elems = snapshots.shape[1]
+    unit_cols = snapshots.shape[2] // n
+    beams = beam_table.shape[0]
+    half_cols, quarter = unit_cols // 2, unit_cols // 4
+    units = jnp.arange(n, dtype=jnp.int32)
+    frequency, band_size, selector = jax.vmap(lambda u: band_of(band_len, u, n))(units)
+    f32, sem = jnp.float32, pltpu.SemaphoreType.DMA
+    raw = (2, local_elems)
+    vmem, hbm, smem = (pl.BlockSpec(memory_space=m) for m in (pltpu.VMEM, pl.ANY, pltpu.SMEM))
+    formed, power = pl.pallas_call(
+        functools.partial(kernel, n),
+        out_shape=(
+            jax.ShapeDtypeStruct((unit_cols, 2 * beams), f32),
+            jax.ShapeDtypeStruct((n, 8, beams), f32),
+        ),
+        in_specs=[smem, hbm, vmem, vmem, vmem],
+        out_specs=(vmem, vmem),
+        scratch_shapes=[
+            pltpu.VMEM((3 * beams, delays.shape[1]), jnp.bfloat16),
+            pltpu.VMEM((8, beams, local_elems), f32),
+            pltpu.VMEM((4, 4) + raw + (half_cols,), f32),
+            pltpu.VMEM((2, 3, 2) + raw + (half_cols,), f32),
+            pltpu.VMEM((2, 2, 2) + raw + (quarter,), f32),
+            pltpu.VMEM((4, 2, 2 * beams, quarter), f32),
+            pltpu.VMEM((3, 2, 2, 2 * beams, quarter), f32),
+            pltpu.VMEM((2, 2 * beams, quarter), f32),
+            pltpu.VMEM((2, 2, 2 * beams, quarter), f32),
+            pltpu.VMEM((2, 2, 2, 2 * beams, quarter), f32),
+            pltpu.VMEM((2, 2 * beams, quarter), f32),
+            pltpu.VMEM((n, 8, beams), f32),
+            sem((4,)), sem((3, 2)),
+            sem((4,)), sem((4,)), sem((3, 2)), sem((3, 2)),
+            sem((2, 4)), sem((2, 4)), sem((2, 2, 2)), sem((2, 2, 2)),
+            sem((2, 2, 2)), sem((2, 2, 2)), sem((2,)), sem((2,)),
+            sem((2, 2)), sem((2, 2)), sem((2,)), sem((2,)),
+            sem((n,)), sem((n,)),
+        ],
+        compiler_params=pltpu.CompilerParams(
+            collective_id=0, has_side_effects=True, vmem_limit_bytes=62 * 1024 * 1024
+        ),
+    )(
+        frequency, snapshots, delays,
+        element_order.reshape(n, 1, local_elems), beam_table.reshape(beams, 1),
+    )
+    row_unit = (lax.axis_index("elem") + n - units) % n
+    share = selector / (band_size.astype(f32) * unit_cols)[:, None]
+    summed = jnp.sum(share[row_unit][:, :, None] * power[:, 0][:, None, :], axis=0)
+    decibels = 10.0 * jnp.log10(summed + epsilon)
+    return (formed.reshape(unit_cols, 2, beams), decibels)
+
+
+def fits(mesh):
+    return mesh.shape["elem"] == SIDE * SIDE * RING
 
 
 def steering(delays, element_order, beam_table, frequency):
@@ -67,8 +428,10 @@
 
 
 def solution(mesh):
+    n = mesh.shape["elem"]
+    body = functools.partial(local_ring, n) if fits(mesh) else local
     return jax.shard_map(
-        local,
+        body,
         mesh=mesh,
         in_specs=(P(None, ("groups", "elem"), None), P(), P("groups"), P("groups"), P()),
         out_specs=(P("elem", None, "groups"), P(None, "groups")),

time: 489 us -> 229 us (0.47)
  waiting for transfers between devices: 264 us -> 0 us
  Pallas kernels: 0 us -> 219 us
  blocking collectives: 98.8 us -> 0 us
  local copies, waits for them, and re-layouts: 64.4 us -> 6.47 us
  matrix products: 33 us -> 0 us
  other arithmetic: 17.6 us -> 3.1 us
  starting transfers between devices: 7.6 us -> 0 us
    all_to_all x1 -> x0, waiting for transfers between devices: 264 us -> none  [local(): lax.all_to_all(divided, 'elem', split_axis=2, concat_axis=1, tiled=True)]
    pallas_call x0 -> x1, Pallas kernels: none -> 219 us  [local_ring(): pl.pallas_call(functools.partial(kernel, n), out_shape=(jax.ShapeDtypeStr...]
    psum x1 -> x0, blocking collectives: 98.8 us -> none  [local(): summed = lax.psum(partial_value, 'elem')]
    dot_general x1 -> x0, matrix products: 33 us -> none  [project(): lax.dot_general(stacked, weights, (((0,), (0,)), ((), ())), precision=lax...]
    unnamed x12 -> x1, local copies, waits for them, and re-layouts: 21.9 us -> 0.01 us
    all_to_all x1 -> x0, local copies, waits for them, and re-layouts: 18 us -> none  [local(): lax.all_to_all(divided, 'elem', split_axis=2, concat_axis=1, tiled=True)]
    neg x1 -> x0, other arithmetic: 10.9 us -> none  [steering(): lower_rows = jnp.concatenate([-sines.T, cosines.T], axis=1)]
    gather x2 -> x1, local copies, waits for them, and re-layouts: 11.3 us -> 0.56 us  [local_ring(): share[row_unit][:, :, None] * power[:, 0][:, None, :]]
  transfers between devices with their start and end apart: 1 -> 0, of which waited for: 1 -> 0; matrix products, arithmetic and copies ran while one was open for 6% -> 0% of each run, Pallas kernels for 0% -> 0%
where the time goes in v1:
time: 229 us
  Pallas kernels  219 us (96%)
  local copies, waits for them, and re-layouts  6.47 us (3%)
  other arithmetic  3.1 us (1%)
    pallas_call x1, Pallas kernels, local_ring(): pl.pallas_call(functools.partial(kernel, n), out_shape=(jax.ShapeDtypeStr...  219 us

profile of v1, /device:TPU:0, one launch (start us, length us, event | category | flops | bytes accessed | tf_op | source)
XLA Modules:
  0.0 229.1 jit_solution(7113783830947507600)
XLA Ops:
  0.6 0.8 reduce-window.8
  1.5 0.1 convert_reduce_fusion
  1.6 0.8 select_reduce_fusion.1
  2.4 0.5 convert_multiply_fusion
  2.9 0.1 convert_divide_fusion
  3.0 0.6 gather_fusion
  3.6 1.5 copy.8.table
  5.1 218.9 %shard_map.68 = (f32[1024,512]{1,0:T(8,128)}, f32[16,8,256]{2,1,0:T(8,128)}) custom-call(f32[16]{0:T(128)} %get-tuple-element.9.freq, f32[2,128,16384]{2,1,0:T(8,128)} %x.1, f32[384,2048]{1,0:T(8,128)} %delays.1, s32[16,1,128]{2,1,0:T(1,128)} %bitcast.10, s32[256,1]{1,0:T(8,128)} %copy.8.table), custom_call_target="tpu_custom_call" | custom-call | tf_op jit(solution)/shard_map/pallas_call | solution.py:338
  224.0 0.9 slice.3
  224.9 0.1 multiply_reduce_fusion
  225.0 0.6 log_multiply_fusion
  225.6 3.5 %reshape.95 = f32[1024,2,256]{2,1,0:T(2,128)} reshape(f32[1024,512]{1,0:T(8,128)} %get-tuple-element.4) | data formatting | bytes 4194304 | tf_op jit(solution)/shard_map/reshape | solution.py:377
  (3 shorter events, 0.0 us)

commit v2 on v0

--- a/solution.py
+++ b/solution.py
@@ -1,11 +1,17 @@
+import functools
 import math
 
 import jax
 import jax.numpy as jnp
 from jax import lax
+from jax.experimental import pallas as pl
+from jax.experimental.pallas import tpu as pltpu
 from jax.sharding import PartitionSpec as P
 
 epsilon = 1e-06
+SIDE = 2
+RING = 4
+CHUNKS = 8
 
 
 def band_of(band_len, position, unit_count):
@@ -18,6 +24,411 @@
         unit_count
     )
     return (frequency, band_size, selector.astype(jnp.float32))
+
+
+def sincos(turns):
+    reduced = turns - jnp.floor(turns + 0.5)
+    x = reduced * math.pi
+    q = x * x
+    sin_terms = [(-1.0) ** i / math.factorial(2 * i + 1) for i in range(7)]
+    cos_terms = [(-1.0) ** i / math.factorial(2 * i) for i in range(8)]
+    s = jnp.full_like(q, sin_terms[-1])
+    for term in sin_terms[-2::-1]:
+        s = s * q + term
+    s = s * x
+    c = jnp.full_like(q, cos_terms[-1])
+    for term in cos_terms[-2::-1]:
+        c = c * q + term
+    return 2.0 * s * c, 1.0 - 2.0 * s * s
+
+
+def split2(v):
+    high = v.astype(jnp.bfloat16)
+    return high, (v - high.astype(jnp.float32)).astype(jnp.bfloat16)
+
+
+def split3(v):
+    high = v.astype(jnp.bfloat16)
+    rest = v - high.astype(jnp.float32)
+    middle = rest.astype(jnp.bfloat16)
+    return high, middle, (rest - middle.astype(jnp.float32)).astype(jnp.bfloat16)
+
+
+def kernel(
+    n, freq, x, delays, order, table, out, power,
+    g1, dt, wh, wl, xa, xb, xz, pa, pb, ra, rb, ry2, pw, tot,
+    own_a, own_b, sa_s, sa_r, sb_s, sb_r, sy_s, sy_r, sz_s, sz_r,
+    a_s, a_r, b_s, b_r, y2_s, y2_r, p_s, p_r,
+):
+    me = lax.axis_index("elem")
+    core = me % SIDE
+    y = (me // SIDE) % SIDE
+    z = me // (SIDE * SIDE)
+    upper = z // 2
+    end = z + upper * (RING - 1 - 2 * z)
+    unit_cols = x.shape[2] // n
+    chunk = unit_cols // CHUNKS
+    early = CHUNKS - 1
+    early_cols = early * chunk
+    beams = table.shape[0]
+    scaling = float(delays.shape[1]) ** (-0.5)
+    slots = (3, 2, 1 - end, end)
+
+    def chip(u):
+        return u + upper * (RING - 1 - 2 * u)
+
+    def dev(zz, yy, cc):
+        return (zz * SIDE + yy % SIDE) * SIDE + cc % SIDE
+
+    ahead = dev(chip(end + 1), y, core)
+    beside = dev(chip(1 - end), y, core)
+
+    barrier = pltpu.get_barrier_semaphore()
+
+    def greet(k, carry):
+        pl.semaphore_signal(barrier, inc=1, device_id={"elem": (me + k) % n},
+                            device_id_type=pl.DeviceIdType.MESH)
+        return carry
+
+    lax.fori_loop(1, n, greet, 0)
+    pl.semaphore_wait(barrier, n - 1)
+
+    def remote(src, dst, send, recv, target):
+        return pltpu.make_async_remote_copy(
+            src_ref=src, dst_ref=dst, send_sem=send, recv_sem=recv,
+            device_id={"elem": target}, device_id_type=pl.DeviceIdType.MESH)
+
+    def cols(unit, start, size):
+        return x.at[:, :, pl.ds(pl.multiple_of(unit * unit_cols + start, 128), size)]
+
+    def part(k):
+        return pl.ds(pl.multiple_of(k * chunk, 128), chunk)
+
+    def y_copy(j, k, r):
+        return remote(
+            cols(dev(chip(slots[j]), y + 1, core + r), k * chunk, chunk),
+            xa.at[2 + r, j, :, :, part(k)],
+            sy_s.at[r, j, k], sy_r.at[r, j, k], dev(z, y + 1, core + r))
+
+    def z_copy(j, yr, r):
+        return remote(
+            cols(dev(chip(3 - j), y + yr, core + r), early_cols, chunk), xz.at[j, r, yr],
+            sz_s.at[j, r, yr], sz_r.at[j, r, yr], dev(chip(1 - end), y, core + r))
+
+    def a_copy(j, k):
+        to = j + 3 * end if j < 2 else 2
+        return remote(pa.at[j, k], ra.at[to, k], a_s.at[j, k], a_r.at[to, k],
+                      ahead if j < 2 else beside)
+
+    def a_wait(to, k):
+        remote(pa.at[0, k], ra.at[to, k], a_s.at[0, k], a_r.at[to, k], beside).wait_recv()
+
+    def b_copy(j, yr):
+        return remote(pb.at[j, yr], rb.at[j, yr], b_s.at[j, yr], b_r.at[j, yr],
+                      ahead if j < 2 else beside)
+
+    everyone = [(yr, j, r) for j in range(3) for yr in (1, 0) for r in (0, 1)]
+
+    @pl.when(end == 0)
+    def _():
+        for yr, j, r in everyone:
+            z_copy(j, yr, r).start()
+
+    for j in range(4):
+        def y_start(k, carry, j=j):
+            for r in (0, 1):
+                y_copy(j, k, r).start()
+            return carry
+
+        lax.fori_loop(0, early, y_start, 0)
+
+    ca, cb, la, lb = {}, {}, {}, {}
+    for j in range(4):
+        there = dev(chip(slots[j]), y, core + 1)
+        here = dev(chip(slots[j]), y, core)
+        ca[j] = remote(cols(there, 0, early_cols), xa.at[1, j],
+                       sa_s.at[j], sa_r.at[j], dev(z, y, core + 1))
+        la[j] = pltpu.make_async_copy(cols(here, 0, early_cols), xa.at[0, j], own_a.at[j])
+        ca[j].start()
+        la[j].start()
+        if j > 0:
+            continue
+        for i in range(4):
+            for yr in (1, 0):
+                there = dev(chip(slots[i]), y + yr, core + 1)
+                here = dev(chip(slots[i]), y + yr, core)
+                cb[i, yr] = remote(cols(there, early_cols, chunk), xb.at[1, i, yr],
+                                   sb_s.at[i, yr], sb_r.at[i, yr], dev(z, y, core + 1))
+                lb[i, yr] = pltpu.make_async_copy(
+                    cols(here, early_cols, chunk), xb.at[0, i, yr], own_b.at[i, yr])
+                cb[i, yr].start()
+                lb[i, yr].start()
+
+    beam_hot = jnp.where(
+        lax.broadcasted_iota(jnp.int32, (beams, delays.shape[0]), 1) == table[...], 1.0, 0.0
+    ).astype(jnp.bfloat16)
+    step = 512 if delays.shape[1] % 512 == 0 else delays.shape[1]
+
+    def pick_beams(i, carry):
+        span = pl.ds(pl.multiple_of(i * step, step), step)
+        parts = split3(delays[:, span])
+        rows = [jnp.dot(beam_hot, piece, preferred_element_type=jnp.float32) for piece in parts]
+        for m, piece in enumerate(rows):
+            g1[m * beams:(m + 1) * beams, span] = piece.astype(jnp.bfloat16)
+        return carry
+
+    lax.fori_loop(0, delays.shape[1] // step, pick_beams, 0)
+
+    def pick_elems(s, carry):
+        r, g = s % 2, s // 2
+        u = end + (g // 2) * (1 - 2 * end)
+        q = dev(chip(u), y + g % 2, core + r)
+        row = order[q]
+        hot = jnp.where(
+            lax.broadcasted_iota(jnp.int32, (delays.shape[1], row.shape[1]), 0) == row, 1.0, 0.0
+        ).astype(jnp.bfloat16)
+        got = jnp.dot(g1[...], hot, preferred_element_type=jnp.float32)
+        dt[s] = got[:beams] + got[beams:2 * beams] + got[2 * beams:]
+        return carry
+
+    lax.fori_loop(0, 6, pick_elems, 0)
+    wide = 2 * x.shape[1]
+
+    def weigh(f, sources):
+        for i, s in enumerate(sources):
+            sine, cosine = sincos(f * dt[s])
+            ch, cl = split2(cosine * scaling)
+            sh, sl = split2(sine * scaling)
+            span = slice(i * wide, (i + 1) * wide)
+            wh[:beams, span] = jnp.concatenate([ch, sh], axis=1)
+            wh[beams:, span] = jnp.concatenate([-sh, ch], axis=1)
+            wl[:beams, span] = jnp.concatenate([cl, sl], axis=1)
+            wl[beams:, span] = jnp.concatenate([-sl, cl], axis=1)
+
+    def form(pieces):
+        rows = jnp.concatenate([piece.reshape(wide, chunk) for piece in pieces], axis=0)
+        xh, xl = split2(rows)
+        span = slice(0, wide * len(pieces))
+        dot = functools.partial(jnp.dot, preferred_element_type=jnp.float32)
+        high = wh[:, span]
+        return dot(high, xh) + (dot(high, xl) + dot(wl[:, span], xh))
+
+    def a_slot(j, then):
+        weigh(freq[dev(chip(slots[j]), y, core)], (0, 1, 2, 3))
+        la[j].wait()
+        ca[j].wait_recv()
+
+        def one(k, carry):
+            for r in (0, 1):
+                y_copy(j, k, r).wait_recv()
+            pa[j, k] = form([xa[s, j, :, :, part(k)] for s in range(4)])
+            then(k)
+            return carry
+
+        lax.fori_loop(0, early, one, 0)
+
+    def join(j, to, k):
+        a_wait(to, k)
+        pa[j, k] += ra[to, k]
+
+    def after0(k):
+        @pl.when(end == 0)
+        def _():
+            a_copy(0, k).start()
+
+    def after1(k):
+        @pl.when(end == 0)
+        def _():
+            a_copy(1, k).start()
+
+        @pl.when(end == 1)
+        def _():
+            join(0, 0, k)
+            a_copy(0, k).start()
+
+    def after2(k):
+        @pl.when(end == 1)
+        def _():
+            join(2, 3, k)
+
+        a_copy(2, k).start()
+
+        @pl.when(end == 1)
+        def _():
+            join(1, 1, k)
+            a_copy(1, k).start()
+
+    def emit(got, start):
+        out[pl.ds(pl.multiple_of(start, 128), chunk), :] = got
+        tot[...] += jnp.sum(got * got, axis=0, keepdims=True)
+
+    def after3(k):
+        @pl.when(end == 1)
+        def _():
+            join(3, 4, k)
+
+        a_wait(2, k)
+        emit((pa[3, k] + ra[2, k]).T, k * chunk)
+
+    tot[...] = jnp.zeros_like(tot)
+    a_slot(0, after0)
+
+    for i in range(4):
+        for yr in (1, 0):
+            lb[i, yr].wait()
+            cb[i, yr].wait_recv()
+
+    @pl.when(end == 1)
+    def _():
+        for yr, j, r in everyone:
+            z_copy(j, yr, r).wait_recv()
+
+        def b_joint(t, carry):
+            i, yr = t // 2, 1 - t % 2
+            j = i + i // 2
+            weigh(freq[dev(chip(3 - i), y + yr, core)], (0, 1, 4, 5))
+            pb[j, yr] = form([xb[0, j, yr], xb[1, j, yr], xz[i, 0, yr], xz[i, 1, yr]])
+            return carry
+
+        lax.fori_loop(0, 6, b_joint, 0)
+        for j in (0, 1):
+            for yr in (1, 0):
+                b_copy(j, yr).start()
+
+    def b_end(t, carry):
+        yr = 1 - t
+        weigh(freq[dev(chip(0), y + yr, core)], (0, 1))
+        pb[3 - end, yr] = form([xb[0, 3 - end, yr], xb[1, 3 - end, yr]])
+        return carry
+
+    lax.fori_loop(0, 2, b_end, 0)
+    a_slot(1, after1)
+
+    @pl.when(end == 1)
+    def _():
+        for yr in (1, 0):
+            b_copy(0, yr).wait_recv()
+            pb[2, yr] += rb[0, yr]
+            b_copy(2, yr).start()
+        for yr in (1, 0):
+            b_copy(1, yr).wait_recv()
+            pb[3, yr] += rb[1, yr]
+
+    a_slot(2, after2)
+
+    @pl.when(end == 0)
+    def _():
+        for yr in (1, 0):
+            b_copy(2, yr).wait_recv()
+            pb[3, yr] += rb[2, yr]
+
+    last = remote(pb.at[3, 1], ry2, y2_s, y2_r, dev(z, y + 1, core))
+    last.start()
+    a_slot(3, after3)
+    last.wait_recv()
+    emit((pb[3, 0] + ry2[...]).T, early_cols)
+    both = tot[:, :beams] + tot[:, beams:]
+    pw[0] = jnp.broadcast_to(both, pw.shape[1:])
+
+    def p_copy(k):
+        return remote(pw.at[0], pw.at[k], p_s.at[k], p_r.at[k], (me + k) % n)
+
+    def p_start(k, carry):
+        p_copy(k).start()
+        return carry
+
+    def p_wait(k, carry):
+        p_copy(k).wait()
+        return carry
+
+    lax.fori_loop(1, n, p_start, 0)
+    last.wait_send()
+    for j in range(4):
+        ca[j].wait_send()
+        for yr in (1, 0):
+            cb[j, yr].wait_send()
+
+        def drain(k, carry, j=j):
+            for r in (0, 1):
+                y_copy(j, k, r).wait_send()
+            if j < 3:
+                a_copy(j, k).wait_send()
+            return carry
+
+        lax.fori_loop(0, early, drain, 0)
+
+    @pl.when(end == 0)
+    def _():
+        for yr, j, r in everyone:
+            z_copy(j, yr, r).wait_send()
+
+    @pl.when(end == 1)
+    def _():
+        for j in range(3):
+            for yr in (1, 0):
+                b_copy(j, yr).wait_send()
+
+    lax.fori_loop(1, n, p_wait, 0)
+    power[...] = pw[...]
+
+
+def local_ring(n, snapshots, delays, element_order, beam_table, band_len):
+    local_elems = snapshots.shape[1]
+    unit_cols = snapshots.shape[2] // n
+    beams = beam_table.shape[0]
+    early, chunk = CHUNKS - 1, unit_cols // CHUNKS
+    block = (2 * beams, chunk)
+    units = jnp.arange(n, dtype=jnp.int32)
+    frequency, band_size, selector = jax.vmap(lambda u: band_of(band_len, u, n))(units)
+    f32, sem = jnp.float32, pltpu.SemaphoreType.DMA
+    raw = (2, local_elems)
+    vmem, hbm, smem = (pl.BlockSpec(memory_space=m) for m in (pltpu.VMEM, pl.ANY, pltpu.SMEM))
+    formed, power = pl.pallas_call(
+        functools.partial(kernel, n),
+        out_shape=(
+            jax.ShapeDtypeStruct((unit_cols, 2 * beams), f32),
+            jax.ShapeDtypeStruct((n, 8, beams), f32),
+        ),
+        in_specs=[smem, hbm, vmem, vmem, vmem],
+        out_specs=(vmem, vmem),
+        scratch_shapes=[
+            pltpu.VMEM((3 * beams, delays.shape[1]), jnp.bfloat16),
+            pltpu.VMEM((6, beams, local_elems), f32),
+            pltpu.VMEM((2 * beams, 8 * local_elems), jnp.bfloat16),
+            pltpu.VMEM((2 * beams, 8 * local_elems), jnp.bfloat16),
+            pltpu.VMEM((4, 4) + raw + (early * chunk,), f32),
+            pltpu.VMEM((2, 4, 2) + raw + (chunk,), f32),
+            pltpu.VMEM((3, 2, 2) + raw + (chunk,), f32),
+            pltpu.VMEM((4, early) + block, f32),
+            pltpu.VMEM((4, 2) + block, f32),
+            pltpu.VMEM((5, early) + block, f32),
+            pltpu.VMEM((3, 2) + block, f32),
+            pltpu.VMEM(block, f32),
+            pltpu.VMEM((n, 8, beams), f32),
+            pltpu.VMEM((1, 2 * beams), f32),
+            sem((4,)), sem((4, 2)),
+            sem((4,)), sem((4,)), sem((4, 2)), sem((4, 2)),
+            sem((2, 4, early)), sem((2, 4, early)), sem((3, 2, 2)), sem((3, 2, 2)),
+            sem((3, early)), sem((5, early)), sem((3, 2)), sem((3, 2)),
+            sem, sem,
+            sem((n,)), sem((n,)),
+        ],
+        compiler_params=pltpu.CompilerParams(
+            collective_id=0, has_side_effects=True, vmem_limit_bytes=62 * 1024 * 1024
+        ),
+    )(
+        frequency, snapshots, delays,
+        element_order.reshape(n, 1, local_elems), beam_table.reshape(beams, 1),
+    )
+    row_unit = (lax.axis_index("elem") + n - units) % n
+    share = selector / (band_size.astype(f32) * unit_cols)[:, None]
+    summed = jnp.sum(share[row_unit][:, :, None] * power[:, 0][:, None, :], axis=0)
+    decibels = 10.0 * jnp.log10(summed + epsilon)
+    return (formed.reshape(unit_cols, 2, beams), decibels)
+
+
+def fits(mesh):
+    return mesh.shape["elem"] == SIDE * SIDE * RING
 
 
 def steering(delays, element_order, beam_table, frequency):
@@ -67,8 +478,10 @@
 
 
 def solution(mesh):
+    n = mesh.shape["elem"]
+    body = functools.partial(local_ring, n) if fits(mesh) else local
     return jax.shard_map(
-        local,
+        body,
         mesh=mesh,
         in_specs=(P(None, ("groups", "elem"), None), P(), P("groups"), P("groups"), P()),
         out_specs=(P("elem", None, "groups"), P(None, "groups")),

time: 489 us -> 191 us (0.39)
  waiting for transfers between devices: 264 us -> 0 us
  Pallas kernels: 0 us -> 181 us
  blocking collectives: 98.8 us -> 0 us
  local copies, waits for them, and re-layouts: 64.4 us -> 6.47 us
  matrix products: 33 us -> 0 us
  other arithmetic: 17.6 us -> 3.1 us
  starting transfers between devices: 7.6 us -> 0 us
    all_to_all x1 -> x0, waiting for transfers between devices: 264 us -> none  [local(): lax.all_to_all(divided, 'elem', split_axis=2, concat_axis=1, tiled=True)]
    pallas_call x0 -> x1, Pallas kernels: none -> 181 us  [local_ring(): pl.pallas_call(functools.partial(kernel, n), out_shape=(jax.ShapeDtypeStr...]
    psum x1 -> x0, blocking collectives: 98.8 us -> none  [local(): summed = lax.psum(partial_value, 'elem')]
    dot_general x1 -> x0, matrix products: 33 us -> none  [project(): lax.dot_general(stacked, weights, (((0,), (0,)), ((), ())), precision=lax...]
    unnamed x12 -> x1, local copies, waits for them, and re-layouts: 21.9 us -> 0.01 us
    all_to_all x1 -> x0, local copies, waits for them, and re-layouts: 18 us -> none  [local(): lax.all_to_all(divided, 'elem', split_axis=2, concat_axis=1, tiled=True)]
    neg x1 -> x0, other arithmetic: 10.9 us -> none  [steering(): lower_rows = jnp.concatenate([-sines.T, cosines.T], axis=1)]
    gather x2 -> x1, local copies, waits for them, and re-layouts: 11.3 us -> 0.56 us  [local_ring(): share[row_unit][:, :, None] * power[:, 0][:, None, :]]
  transfers between devices with their start and end apart: 1 -> 0, of which waited for: 1 -> 0; matrix products, arithmetic and copies ran while one was open for 6% -> 0% of each run, Pallas kernels for 0% -> 0%
where the time goes in v2:
time: 191 us
  Pallas kernels  181 us (95%)
  local copies, waits for them, and re-layouts  6.47 us (3%)
  other arithmetic  3.1 us (2%)
    pallas_call x1, Pallas kernels, local_ring(): pl.pallas_call(functools.partial(kernel, n), out_shape=(jax.ShapeDtypeStr...  181 us

profile of v2, /device:TPU:0, one launch (start us, length us, event | category | flops | bytes accessed | tf_op | source)
XLA Modules:
  0.0 191.1 jit_solution(5903704836650156542)
XLA Ops:
  0.6 0.8 reduce-window.8
  1.5 0.1 convert_reduce_fusion
  1.6 0.8 select_reduce_fusion.1
  2.4 0.5 convert_multiply_fusion
  2.9 0.1 convert_divide_fusion
  3.0 0.6 gather_fusion
  3.6 1.5 copy.8.table
  5.1 180.9 %shard_map.68 = (f32[1024,512]{1,0:T(8,128)}, f32[16,8,256]{2,1,0:T(8,128)}) custom-call(f32[16]{0:T(128)} %get-tuple-element.9.freq, f32[2,128,16384]{2,1,0:T(8,128)} %x.1, f32[384,2048]{1,0:T(8,128)} %delays.1, s32[16,1,128]{2,1,0:T(1,128)} %bitcast.10, s32[256,1]{1,0:T(8,128)} %copy.8.table), custom_call_target="tpu_custom_call" | custom-call | tf_op jit(solution)/shard_map/pallas_call | solution.py:386
  186.0 0.9 slice.3
  186.9 0.1 multiply_reduce_fusion
  187.0 0.6 log_multiply_fusion
  187.6 3.5 %reshape.95 = f32[1024,2,256]{2,1,0:T(2,128)} reshape(f32[1024,512]{1,0:T(8,128)} %get-tuple-element.4) | data formatting | bytes 4194304 | tf_op jit(solution)/shard_map/reshape | solution.py:427
  (3 shorter events, 0.0 us)
